TPU v7x, 256 devices: a 8x8x2 block of a 8x8x16 slice. The times are simulated.
256 devices in a mesh: grp: 2 (over z), pool: 128 (over y, x, core).
Axes of the slice: x: 8, y: 8, z: 2, core: 2. Of those that a mesh axis runs over, the one named last changes fastest.
The devices are a block of a 8x8x16 slice.
Arguments:
- query: bfloat16 [256, 4096], P(('grp', 'pool')), parts along dimension 0, may hold values from -6 to 6
- kv_pool: bfloat16 [16384, 2, 16, 512], P(('grp', 'pool')), parts along dimension 0, may hold values from -6 to 6
- holder_table: int32 [256, 128], P(('grp', 'pool')), parts along dimension 0, may hold values from 0 to 127, as said below
- slot_table: int32 [256, 128], P(('grp', 'pool')), parts along dimension 0, may hold values from 0 to 63
- lengths: int32 [256], P(('grp', 'pool')), parts along dimension 0, may hold values from 96 to 128, as said below
- out_weight: bfloat16 [4096, 8192], P('pool'), may hold values from -5 to 5
Outputs:
- mixed: bfloat16 [256, 8192], P(('grp', 'pool')), parts along dimension 0
There are 2 independent parts, one for each index of `grp`. A program takes and returns all parts, laid end to end along the dimension named above; an argument that names none is the same for every part. Nothing has to cross between parts.
Inputs may be any that keep to these rules, and one draw needn't show every extreme that they name: `holder_table`: entry [r, j] is the index along pool of the device holding block j of request r. Of one request's 128 blocks at most 2 have the same holder, and some holder has exactly 2 of the request's first 96 blocks. Request r's live blocks are 0 to lengths[r] - 1; some request has 128.
All inputs are finite; a program needn't handle non-finite values.
Results may differ from a plain program's by a relative error of at most 0.0053.
Values may be sent and summed in bfloat16 or wider, within the bound.
No kernel may reach another device: no remote copies, remote signals or barrier semaphores. Data moves between devices by JAX's collectives and lax.ppermute only.
A program may use at most 64 MiB of HBM per device.

v0:
```python
import math
import jax
import jax.numpy as jnp
from jax import lax
from jax.sharding import Mesh
from jax.sharding import PartitionSpec as P

H = 32
KVH = 4
HD = 128
POOL = ("pool_0", "pool_1", "pool_2")
GRP_POOL = ("grp", "pool_0", "pool_1", "pool_2")
lowest = -1e30


def side_by_side(arrays, axis, dim, along):
    columns = [a.reshape(*a.shape[:along], -1) for a in arrays]
    both = jnp.concatenate(columns, axis=along)
    out, at, outs = (lax.all_gather(both, axis, axis=dim, tiled=True), 0, [])
    for a, column in zip(arrays, columns):
        piece = out[..., at : at + column.shape[along]]
        outs.append(piece.reshape(*piece.shape[:along], *a.shape[along:]))
        at += column.shape[along]
    return tuple(outs)


def side_by_side_2(arrays, axis, split_dim, concat_dim, along):
    widths = [a.shape[along] for a in arrays]
    both = jnp.concatenate(arrays, axis=along)
    out = lax.all_to_all(both, axis, split_axis=split_dim, concat_axis=concat_dim, tiled=True)
    return tuple(jnp.split(out, [sum(widths[:k]) for k in range(1, len(widths))], axis=along))


def laid_out(pieces, dim):
    lengths = list(pieces.shape[1:])
    lengths[dim] *= pieces.shape[0]
    return jnp.moveaxis(pieces, 0, dim).reshape(lengths)


def gather_in_order(x, axes, order):
    pieces = x[None]
    for k in order:
        pieces = lax.all_gather(pieces, axes[k], axis=0, tiled=True)
    block = [lax.axis_size(axes[k]) for k in reversed(order)]
    pieces = pieces.reshape(*block, *x.shape)
    turned = sorted(range(len(order)), key=lambda place: order[len(order) - 1 - place])
    return pieces.transpose(*turned, *range(len(order), pieces.ndim)).reshape(-1, *x.shape)


def gathered_by_axis(x, axes, order, dim):
    return laid_out(gather_in_order(x, axes, order), dim)


def block_partials(query_heads, kv_blocks):
    head_dim = query_heads.shape[-1]
    kv_heads = query_heads.shape[1]
    block_len = kv_blocks.shape[3]
    block_shape = kv_blocks.shape[:2] + (block_len, kv_heads, head_dim)
    key_part = kv_blocks[:, :, 0].reshape(block_shape)
    value_part = kv_blocks[:, :, 1].reshape(block_shape)
    scores = jnp.einsum(
        "agqd,acbgd->acgqb", query_heads, key_part, preferred_element_type=jnp.float32
    )
    scores = scores * (1.0 / math.sqrt(head_dim))
    maxima = jnp.max(scores, axis=-1)
    shifted = jnp.exp(scores - maxima[..., None])
    totals = jnp.sum(shifted, axis=-1)
    outputs = jnp.einsum(
        "acgqb,acbgd->acgqd",
        shifted.astype(jnp.bfloat16),
        value_part,
        preferred_element_type=jnp.float32,
    )
    return (maxima, outputs, totals)


def merge_blocks(maxima, outputs, totals, live_mask, axis_pos):
    peak_score = jnp.max(jnp.where(live_mask, maxima, lowest), axis=axis_pos, keepdims=True)
    factor = jnp.exp(jnp.where(live_mask, maxima - peak_score, lowest))
    numerator = jnp.sum(factor[..., None] * outputs, axis=axis_pos)
    denominator = jnp.sum(factor * totals, axis=axis_pos)
    return (jnp.squeeze(peak_score, axis_pos), numerator, denominator)


def per_device(query, kv_pool, holder_table, slot_table, lengths, out_weight):
    pool_size = lax.axis_size(POOL)
    my_index = lax.axis_index(POOL)
    max_blocks = holder_table.shape[1]
    capacity = 2 * max_blocks // pool_size
    groups = H // KVH
    all_holders, all_slots, all_lengths = side_by_side(
        (holder_table, slot_table, lengths), POOL, 0, 1
    )
    cap_iota = jnp.arange(capacity, dtype=jnp.int32)
    block_iota = jnp.arange(max_blocks, dtype=jnp.int32)
    held_here = all_holders == my_index
    rank_here = jnp.cumsum(held_here.astype(jnp.int32), axis=1) - 1
    pick_hot = held_here[:, None, :] & (rank_here[:, None, :] == cap_iota[None, :, None])
    pick_slot = jnp.sum(jnp.where(pick_hot, all_slots[:, None, :], 0), axis=-1)
    pick_block = jnp.sum(jnp.where(pick_hot, block_iota[None, None, :], 0), axis=-1)
    send_live = jnp.any(pick_hot, axis=-1) & (pick_block < all_lengths[:, None])
    send_blocks = kv_pool[pick_slot]
    all_queries = lax.all_gather(query, POOL, axis=0, tiled=True)
    maxima, outputs, totals = block_partials(
        all_queries.reshape(pool_size, KVH, groups, HD), send_blocks
    )
    part_peak, part_numer, part_denom = merge_blocks(
        maxima, outputs, totals, send_live[:, :, None, None], 1
    )
    got_peak, got_numer, got_denom = side_by_side_2(
        (
            part_peak.reshape(pool_size, H),
            part_numer.reshape(pool_size, H * HD),
            part_denom.reshape(pool_size, H),
        ),
        POOL,
        0,
        0,
        1,
    )
    peak_score, numerator, denominator = merge_blocks(
        got_peak.reshape(pool_size, KVH, groups),
        got_numer.reshape(pool_size, KVH, groups, HD),
        got_denom.reshape(pool_size, KVH, groups),
        True,
        0,
    )
    attention = (numerator / denominator[..., None]).reshape(1, H * HD).astype(jnp.bfloat16)
    weight_block = lax.all_to_all(out_weight, POOL, split_axis=1, concat_axis=0, tiled=True)
    every_request = gathered_by_axis(attention, POOL, (0, 1, 2), 0)
    column_part = jnp.dot(every_request, weight_block, preferred_element_type=jnp.float32).astype(
        jnp.bfloat16
    )
    mixed = lax.all_to_all(column_part, POOL, split_axis=0, concat_axis=1, tiled=True)
    return mixed


def solution(mesh):
    torus = Mesh(
        mesh.devices.reshape(mesh.shape["grp"], 8, 8, 2), ("grp", "pool_0", "pool_1", "pool_2")
    )
    return jax.shard_map(
        per_device,
        mesh=torus,
        in_specs=(
            P(GRP_POOL, None),
            P(GRP_POOL, None, None, None),
            P(GRP_POOL, None),
            P(GRP_POOL, None),
            P(GRP_POOL),
            P(POOL, None),
        ),
        out_specs=P(GRP_POOL, None),
        check_vma=False,
    )
```

profile of v0, /device:TPU:513, one launch (start us, length us, event | category | flops | bytes accessed | tf_op | source)
XLA Modules:
  0.0 358.0 jit_solution(3321120689761888645)
XLA Ops:
  8.7 67.2 %all-gather = s32[128,1,257]{2,1,0:T(1,128)S(1)} all-gather(s32[1,1,257]{2,1,0:T(1,128)S(1)} %add_bitcast_fusion), channel_id=1, replica_groups=mesh['grp'=2,'pool_0'=8,'pool_1'=8,'pool_2'=2] {'pool_0','pool_1','pool_2'}, dimensions={0}, use_global_device_ids=true | all-gather | bytes 132612 | tf_op jit(solution)/shard_map/all_gather | solution.py:19
  77.0 8.8 %gather_fusion = bf16[256,2,16,512]{3,2,1,0:T(8,128)(2,1)} fusion(bf16[64,2,16,512]{3,2,1,0:T(8,128)(2,1)S(1)} %copy-done, s32[1024]{0:T(1024)S(1)} %pad_clamp_fusion), kind=kCustom, calls=%fused_computation | custom fusion | bytes 16778240 | tf_op jit(solution)/shard_map/gather | solution.py:102
  85.8 6.4 %fusion.10 = (bf16[128,2,1,16,512]{4,3,2,1,0:T(8,128)(2,1)}, bf16[128,2,1,16,512]{4,3,2,1,0:T(8,128)(2,1)}) fusion(bf16[128,2,2,16,512]{4,3,2,1,0:T(8,128)(2,1)} %bitcast.61), kind=kLoop, calls=%fused_computation.34 | loop fusion | bytes 16777216 | tf_op jit(solution)/shard_map/slice | solution.py:60
  92.3 7.9 %copy.129 = bf16[128,2,1,16,512]{0,4,3,1,2:T(8,128)(2,1)} copy(bf16[128,2,1,16,512]{4,3,2,1,0:T(8,128)(2,1)} %get-tuple-element.12) | data formatting | bytes 8388608 | tf_op jit(solution)/shard_map/slice | solution.py:59
  100.2 8.0 %copy.131 = bf16[128,2,16,4,128]{4,2,1,3,0:T(8,128)(2,1)} copy(bf16[128,2,16,4,128]{0,4,3,2,1:T(8,128)(2,1)} %bitcast.62) | data formatting | bytes 8388608 | tf_op jit(solution)/shard_map/reshape;squeeze | solution.py:59
  108.2 7.9 %copy.138 = bf16[128,2,1,16,512]{0,4,3,1,2:T(8,128)(2,1)} copy(bf16[128,2,1,16,512]{4,3,2,1,0:T(8,128)(2,1)} %get-tuple-element.11) | data formatting | bytes 8388608 | tf_op jit(solution)/shard_map/slice | solution.py:60
  116.0 7.9 %copy.140 = bf16[128,2,16,4,128]{4,2,3,1,0:T(8,128)(2,1)} copy(bf16[128,2,16,4,128]{0,4,3,2,1:T(8,128)(2,1)} %bitcast.63) | data formatting | bytes 8388608 | tf_op jit(solution)/shard_map/reshape;squeeze | solution.py:60
  124.1 5.0 %copy.130 = bf16[128,1,4096]{0,2,1:T(8,128)(2,1)S(1)} copy(bf16[128,1,4096]{2,1,0:T(2,128)(2,1)} %all-gather.7.cloned.1.call-done) | data formatting | bytes 2097152 | tf_op jit(solution)/shard_map/all_gather | solution.py:103
  130.2 14.0 %fusion.11 = f32[128,4,2,16,8]{3,4,2,1,0:T(8,128)} fusion(bf16[128,2,16,4,128]{4,2,1,3,0:T(8,128)(2,1)} %copy.131, bf16[128,4,8,128,1]{3,2,4,1,0:T(8,128)(2,1)S(1)} %copy.150), kind=kOutput, calls=%fused_computation.36 | convolution fusion | flops 33554432 | bytes 5767168 | tf_op jit(solution)/shard_map/agqd,acbgd->acgqb/dot_general | solution.py:61
  144.2 3.7 %copy.133 = f32[128,4,2,16,8]{0,3,4,1,2:T(8,128)S(1)} copy(f32[128,4,2,16,8]{3,4,2,1,0:T(8,128)} %fusion.11) | data formatting | bytes 1048576 | tf_op jit(solution)/shard_map/agqd,acbgd->acgqb/dot_general | solution.py:61
  148.5 3.0 copy.139
  151.4 4.9 %multiply_reduce_fusion = f32[128,4,8,128]{3,2,1,0:T(8,128)} fusion(bf16[128,2,4,8,16]{4,3,2,1,0:T(8,128)(2,1)S(1)} %copy.139, bf16[128,2,16,4,128]{4,2,3,1,0:T(8,128)(2,1)} %copy.140, f32[128,2,4,8]{3,2,1,0:T(4,128)S(1)} %copy.137), kind=kOutput, calls=%fused_computation.1 | convolution fusion | flops 35127296 | bytes 6586368 | tf_op jit(solution)/shard_map/acgqb,acbgd->acgqd/dot_general | solution.py:68
  156.4 2.0 copy.153
  159.8 5.7 %copy.144 = f32[128,1,4160]{2,1,0:T(1,128)} copy(f32[128,1,4160]{0,2,1:T(8,128)} %maximum_bitcast_fusion) | data formatting | bytes 4259840 | tf_op jit(solution)/shard_map/all_to_all | solution.py:30
  165.5 60.6 %all_to_all.47 = f32[128,1,4160]{2,1,0:T(1,128)} all-to-all(f32[128,1,4160]{2,1,0:T(1,128)} %copy.144), channel_id=1, replica_groups=mesh['grp'=2,'pool_0'=8,'pool_1'=8,'pool_2'=2] {'pool_0','pool_1','pool_2'}, dimensions={0} | all-to-all | bytes 4259840 | tf_op jit(solution)/shard_map/all_to_all | solution.py:30
  226.1 5.7 %copy.145 = f32[128,1,4160]{0,2,1:T(8,128)} copy(f32[128,1,4160]{2,1,0:T(1,128)} %all_to_all.47) | data formatting | bytes 4259840 | tf_op jit(solution)/shard_map/all_to_all | solution.py:30
  234.5 2.2 fusion
  236.9 18.6 %all_gather.17 = bf16[8,1,4096]{2,1,0:T(2,128)(2,1)S(1)} all-gather(bf16[1,1,4096]{2,1,0:T(2,128)(2,1)S(1)} %divide_convert_fusion), channel_id=1, replica_groups=mesh['grp'=2,'pool_0'=8,'pool_1'=8,'pool_2'=2] {'pool_0'}, dimensions={0}, use_global_device_ids=true | all-gather | bytes 73728 | tf_op jit(solution)/shard_map/all_gather | solution.py:43
  255.6 21.6 %all_gather.18 = bf16[64,1,4096]{2,0,1:T(8,128)(2,1)} all-gather(bf16[8,1,4096]{2,0,1:T(8,128)(2,1)S(1)} %copy.146), channel_id=1, replica_groups=mesh['grp'=2,'pool_0'=8,'pool_1'=8,'pool_2'=2] {'pool_1'}, dimensions={0}, use_global_device_ids=true | all-gather | bytes 589824 | tf_op jit(solution)/shard_map/all_gather | solution.py:43
  279.6 42.9 %all_to_all.48 = bf16[128,2,1024]{2,1,0:T(2,128)(2,1)S(1)} all-to-all(bf16[128,2,1024]{2,1,0:T(2,128)(2,1)S(1)} %reshape.145), channel_id=1, replica_groups=mesh['grp'=2,'pool_0'=8,'pool_1'=8,'pool_2'=2] {'pool_0','pool_1','pool_2'}, dimensions={0} | all-to-all | bytes 1048576 | tf_op jit(solution)/shard_map/all_to_all | solution.py:129
  323.2 3.5 copy.147
  326.7 2.3 reshape_reshape.3
  328.9 1.8 fusion.1
  330.8 19.4 %all_to_all.49 = bf16[128,1,64]{2,1,0:T(2,128)(2,1)S(1)} all-to-all(bf16[128,1,64]{2,1,0:T(2,128)(2,1)S(1)} %copy.149), channel_id=1, replica_groups=mesh['grp'=2,'pool_0'=8,'pool_1'=8,'pool_2'=2] {'pool_0','pool_1','pool_2'}, dimensions={0} | all-to-all | bytes 32768 | tf_op jit(solution)/shard_map/all_to_all | solution.py:134
  (51 shorter events, 12.7 us)
Async XLA Ops:
  6.5 70.5 %copy-start = (bf16[64,2,16,512]{3,2,1,0:T(8,128)(2,1)S(1)}, bf16[64,2,16,512]{3,2,1,0:T(8,128)(2,1)}, u32[]{:S(2)}) copy-start(bf16[64,2,16,512]{3,2,1,0:T(8,128)(2,1)} %param.7) | copy-start | bytes 6291460
  6.6 117.6 %all-gather.7.cloned.1.call-start = ((), (), s32[]{:S(2)}) async-start(), calls=%async_computation.4 | async-start | bytes 2113536 | tf_op jit(solution)/shard_map/all_gather | solution.py:103
  7.3 315.9 %all-gather.5.cloned.1.call-start = ((), (), s32[]{:S(2)}) async-start(), calls=%async_computation.3 | async-start | bytes 1572864 | tf_op jit(solution)/shard_map/all_gather | solution.py:43
  231.8 45.5 %copy-start.2 = (bf16[32,8192]{1,0:T(8,128)(2,1)S(1)}, bf16[32,8192]{1,0:T(8,128)(2,1)}, u32[]{:S(2)}) copy-start(bf16[32,8192]{1,0:T(8,128)(2,1)} %param.11) | copy-start | bytes 1572868
  323.2 27.9 %copy-start.1 = (bf16[64,2,16,512]{3,2,1,0:T(8,128)(2,1)S(1)}, bf16[64,2,16,512]{3,2,1,0:T(8,128)(2,1)}, u32[]{:S(2)}) copy-start(bf16[64,2,16,512]{3,2,1,0:T(8,128)(2,1)} %param.7) | copy-start | bytes 6291460
Sparse Core Ops, SparseCore 0:
  9.9 98.6 all-gather.6
  277.3 31.8 all-gather.4
where the time goes:
time: 360 us; the launch traced here: 358 us
  blocking collectives  230 us (64%)
  local copies, waits for them, and re-layouts  83.9 us (23%)
  matrix products  20.7 us (6%)
  between operations  14.3 us (4%)
  other arithmetic  7.94 us (2%)
    all_gather x1, blocking collectives, side_by_side(): out, at, outs = (lax.all_gather(both, axis, axis=dim, tiled=True), 0, [])  67.2 us
    all_to_all x1, blocking collectives, side_by_side_2(): lax.all_to_all(both, axis, split_axis=split_dim, concat_axis=concat_dim,...  60.6 us
    all_to_all x1, blocking collectives, per_device(): lax.all_to_all(out_weight, POOL, split_axis=1, concat_axis=0, tiled=True)  42.9 us
    all_gather x2, blocking collectives, gather_in_order(): pieces = lax.all_gather(pieces, axes[k], axis=0, tiled=True)  40.2 us
    all_to_all x1, blocking collectives, per_device(): lax.all_to_all(column_part, POOL, split_axis=0, concat_axis=1, tiled=True)  19.4 us
    slice x2, local copies, waits for them, and re-layouts, block_partials(): value_part = kv_blocks[:, :, 1].reshape(block_shape)  14.3 us
    dot_general x1, matrix products, block_partials(): jnp.einsum('agqd,acbgd->acgqb', query_heads, key_part, preferred_element_...  14 us
    all_to_all x2, local copies, waits for them, and re-layouts, side_by_side_2(): lax.all_to_all(both, axis, split_axis=split_dim, concat_axis=concat_dim,...  11.4 us
  transfers between devices with their start and end apart: 2, of which 0 were waited for; matrix products, arithmetic and copies ran while one was open for 14% of the time, Pallas kernels for 0%

commit v1 on v0

--- a/solution.py
+++ b/solution.py
@@ -40,7 +40,9 @@
 def gather_in_order(x, axes, order):
     pieces = x[None]
     for k in order:
-        pieces = lax.all_gather(pieces, axes[k], axis=0, tiled=True)
+        pieces = jnp.concatenate(
+            lax.all_to_all(jnp.stack([pieces] * lax.axis_size(axes[k])), axes[k], 0, 0), axis=0
+        )
     block = [lax.axis_size(axes[k]) for k in reversed(order)]
     pieces = pieces.reshape(*block, *x.shape)
     turned = sorted(range(len(order)), key=lambda place: order[len(order) - 1 - place])

time: 360 us -> 342 us (0.950)
  blocking collectives: 230 us -> 153 us
  waiting for transfers between devices: 0.84 us -> 40.1 us
  starting transfers between devices: 0.06 us -> 17.8 us
    all_gather x2 -> x0, blocking collectives: 40.2 us -> none  [gather_in_order(): pieces = lax.all_gather(pieces, axes[k], axis=0, tiled=True)]
    all_to_all x0 -> x3, waiting for transfers between devices: none -> 39.3 us  [the longest x2 19.9 us: gather_in_order(): lax.all_to_all(jnp.stack([pieces] * lax.axis_size(axes[k])), axes[k], 0, 0)]
    all_to_all x1, blocking collectives: 42.9 us -> 5.97 us  [gather_in_order(): lax.all_to_all(jnp.stack([pieces] * lax.axis_size(axes[k])), axes[k], 0, 0)]
    all_to_all x0 -> x3, starting transfers between devices: none -> 17.8 us  [the longest x1 9.82 us: per_device(): lax.all_to_all(out_weight, POOL, split_axis=1, concat_axis=0, tiled=True)]
  transfers between devices with their start and end apart: 2 -> 4, of which waited for: 0 -> 3; matrix products, arithmetic and copies ran while one was open for 14% -> 15% of each run, Pallas kernels for 0% -> 0%
where the time goes in v1:
time: 342 us; the launch traced here: 340 us
  blocking collectives  153 us (45%)
  local copies, waits for them, and re-layouts  85.5 us (25%)
  waiting for transfers between devices  40.1 us (12%)
  matrix products  20.7 us (6%)
  starting transfers between devices  17.8 us (5%)
  between operations  14.3 us (4%)
  other arithmetic  9.09 us (3%)
    all_gather x1, blocking collectives, side_by_side(): out, at, outs = (lax.all_gather(both, axis, axis=dim, tiled=True), 0, [])  67.2 us
    all_to_all x1, blocking collectives, side_by_side_2(): lax.all_to_all(both, axis, split_axis=split_dim, concat_axis=concat_dim,...  60.6 us
    all_to_all x2, waiting for transfers between devices, gather_in_order(): lax.all_to_all(jnp.stack([pieces] * lax.axis_size(axes[k])), axes[k], 0, 0)  19.9 us
    all_to_all x1, waiting for transfers between devices, per_device(): lax.all_to_all(out_weight, POOL, split_axis=1, concat_axis=0, tiled=True)  19.4 us
    all_to_all x1, blocking collectives, per_device(): lax.all_to_all(column_part, POOL, split_axis=0, concat_axis=1, tiled=True)  19.1 us
    slice x2, local copies, waits for them, and re-layouts, block_partials(): value_part = kv_blocks[:, :, 1].reshape(block_shape)  14.3 us
    dot_general x1, matrix products, block_partials(): jnp.einsum('agqd,acbgd->acgqb', query_heads, key_part, preferred_element_...  14 us
    all_to_all x2, local copies, waits for them, and re-layouts, side_by_side_2(): lax.all_to_all(both, axis, split_axis=split_dim, concat_axis=concat_dim,...  11.4 us
  transfers between devices with their start and end apart: 4, of which 3 were waited for; matrix products, arithmetic and copies ran while one was open for 15% of the time, Pallas kernels for 0%

profile of v1, /device:TPU:513, one launch (start us, length us, event | category | flops | bytes accessed | tf_op | source)
XLA Modules:
  0.0 340.4 jit_solution(5574051132559374880)
XLA Ops:
  8.6 67.2 %all-gather = s32[128,1,257]{2,1,0:T(1,128)S(1)} all-gather(s32[1,1,257]{2,1,0:T(1,128)S(1)} %add_bitcast_fusion), channel_id=1, replica_groups=mesh['grp'=2,'pool_0'=8,'pool_1'=8,'pool_2'=2] {'pool_0','pool_1','pool_2'}, dimensions={0}, use_global_device_ids=true | all-gather | bytes 132612 | tf_op jit(solution)/shard_map/all_gather | solution.py:19
  77.0 8.8 %gather_fusion = bf16[256,2,16,512]{3,2,1,0:T(8,128)(2,1)} fusion(bf16[64,2,16,512]{3,2,1,0:T(8,128)(2,1)S(1)} %copy-done, s32[1024]{0:T(1024)S(1)} %pad_clamp_fusion), kind=kCustom, calls=%fused_computation | custom fusion | bytes 16778240 | tf_op jit(solution)/shard_map/gather | solution.py:104
  85.7 6.4 %fusion.11 = (bf16[128,2,1,16,512]{4,3,2,1,0:T(8,128)(2,1)}, bf16[128,2,1,16,512]{4,3,2,1,0:T(8,128)(2,1)}) fusion(bf16[128,2,2,16,512]{4,3,2,1,0:T(8,128)(2,1)} %bitcast.68), kind=kLoop, calls=%fused_computation.38 | loop fusion | bytes 16777216 | tf_op jit(solution)/shard_map/slice | solution.py:62
  92.2 7.9 %copy.125 = bf16[128,2,1,16,512]{0,4,3,1,2:T(8,128)(2,1)} copy(bf16[128,2,1,16,512]{4,3,2,1,0:T(8,128)(2,1)} %get-tuple-element.12) | data formatting | bytes 8388608 | tf_op jit(solution)/shard_map/slice | solution.py:61
  100.1 8.0 %copy.127 = bf16[128,2,16,4,128]{4,2,1,3,0:T(8,128)(2,1)} copy(bf16[128,2,16,4,128]{0,4,3,2,1:T(8,128)(2,1)} %bitcast.69) | data formatting | bytes 8388608 | tf_op jit(solution)/shard_map/reshape;squeeze | solution.py:61
  108.1 7.9 %copy.134 = bf16[128,2,1,16,512]{0,4,3,1,2:T(8,128)(2,1)} copy(bf16[128,2,1,16,512]{4,3,2,1,0:T(8,128)(2,1)} %get-tuple-element.11) | data formatting | bytes 8388608 | tf_op jit(solution)/shard_map/slice | solution.py:62
  116.0 7.9 %copy.136 = bf16[128,2,16,4,128]{4,2,3,1,0:T(8,128)(2,1)} copy(bf16[128,2,16,4,128]{0,4,3,2,1:T(8,128)(2,1)} %bitcast.70) | data formatting | bytes 8388608 | tf_op jit(solution)/shard_map/reshape;squeeze | solution.py:62
  124.1 5.0 %copy.126 = bf16[128,1,4096]{0,2,1:T(8,128)(2,1)S(1)} copy(bf16[128,1,4096]{2,1,0:T(2,128)(2,1)} %all-gather.4.cloned.1.call-done) | data formatting | bytes 2097152 | tf_op jit(solution)/shard_map/all_gather | solution.py:105
  130.1 14.0 %fusion.12 = f32[128,4,2,16,8]{3,4,2,1,0:T(8,128)} fusion(bf16[128,2,16,4,128]{4,2,1,3,0:T(8,128)(2,1)} %copy.127, bf16[128,4,8,128,1]{3,2,4,1,0:T(8,128)(2,1)S(1)} %copy.145), kind=kOutput, calls=%fused_computation.40 | convolution fusion | flops 33554432 | bytes 5767168 | tf_op jit(solution)/shard_map/agqd,acbgd->acgqb/dot_general | solution.py:63
  144.1 3.7 %copy.129 = f32[128,4,2,16,8]{0,3,4,1,2:T(8,128)S(1)} copy(f32[128,4,2,16,8]{3,4,2,1,0:T(8,128)} %fusion.12) | data formatting | bytes 1048576 | tf_op jit(solution)/shard_map/agqd,acbgd->acgqb/dot_general | solution.py:63
  148.4 3.0 copy.135
  151.4 4.9 %multiply_reduce_fusion = f32[128,4,8,128]{3,2,1,0:T(8,128)} fusion(bf16[128,2,4,8,16]{4,3,2,1,0:T(8,128)(2,1)S(1)} %copy.135, bf16[128,2,16,4,128]{4,2,3,1,0:T(8,128)(2,1)} %copy.136, f32[128,2,4,8]{3,2,1,0:T(4,128)S(1)} %copy.133), kind=kOutput, calls=%fused_computation.1 | convolution fusion | flops 35127296 | bytes 6586368 | tf_op jit(solution)/shard_map/acgqb,acbgd->acgqd/dot_general | solution.py:70
  159.8 5.7 %copy.140 = f32[128,1,4160]{2,1,0:T(1,128)} copy(f32[128,1,4160]{0,2,1:T(8,128)} %maximum_bitcast_fusion) | data formatting | bytes 4259840 | tf_op jit(solution)/shard_map/all_to_all | solution.py:30
  165.5 60.6 %all_to_all.62 = f32[128,1,4160]{2,1,0:T(1,128)} all-to-all(f32[128,1,4160]{2,1,0:T(1,128)} %copy.140), channel_id=1, replica_groups=mesh['grp'=2,'pool_0'=8,'pool_1'=8,'pool_2'=2] {'pool_0','pool_1','pool_2'}, dimensions={0} | all-to-all | bytes 4259840 | tf_op jit(solution)/shard_map/all_to_all | solution.py:30
  226.1 5.7 %copy.141 = f32[128,1,4160]{0,2,1:T(8,128)} copy(f32[128,1,4160]{2,1,0:T(1,128)} %all_to_all.62) | data formatting | bytes 4259840 | tf_op jit(solution)/shard_map/all_to_all | solution.py:30
  239.1 4.3 %all-to-all-start.1 = ((bf16[8,2,2048]{2,1,0:T(2,128)(2,1)}), bf16[8,2,2048]{2,1,0:T(2,128)(2,1)S(1)}, u32[]{:S(2)}, u32[]{:S(2)}) async-start(bf16[8,2,2048]{2,1,0:T(2,128)(2,1)} %reshape.140), calls=%async_computation.1 | async-start | bytes 131072 | tf_op jit(solution)/shard_map/all_to_all | solution.py:44
  246.6 4.0 %all-to-all-done.1 = bf16[8,2,2048]{2,1,0:T(2,128)(2,1)S(1)} async-done(((bf16[8,2,2048]{2,1,0:T(2,128)(2,1)}), bf16[8,2,2048]{2,1,0:T(2,128)(2,1)S(1)}, u32[]{:S(2)}, u32[]{:S(2)}) %all-to-all-start.1) | async-done | bytes 65568 | tf_op jit(solution)/shard_map/all_to_all | solution.py:44
  250.6 9.8 %all-to-all-start.4 = ((bf16[128,2,1024]{2,1,0:T(2,128)(2,1)}), bf16[128,2,1024]{2,1,0:T(2,128)(2,1)S(1)}, u32[]{:S(2)}, u32[]{:S(2)}) async-start(bf16[128,2,1024]{2,1,0:T(2,128)(2,1)} %reshape.142), calls=%async_computation.4 | async-start | bytes 1048576 | tf_op jit(solution)/shard_map/all_to_all | solution.py:131
  260.6 19.4 %all-to-all-done.4 = bf16[128,2,1024]{2,1,0:T(2,128)(2,1)S(1)} async-done(((bf16[128,2,1024]{2,1,0:T(2,128)(2,1)}), bf16[128,2,1024]{2,1,0:T(2,128)(2,1)S(1)}, u32[]{:S(2)}, u32[]{:S(2)}) %all-to-all-start.4) | async-done | bytes 524320 | tf_op jit(solution)/shard_map/all_to_all | solution.py:131
  280.8 3.7 %all-to-all-start.2 = ((bf16[8,8,1,4096]{3,1,2,0:T(8,128)(2,1)}), bf16[8,8,1,4096]{3,1,2,0:T(8,128)(2,1)S(1)}, u32[]{:S(2)}, u32[]{:S(2)}) async-start(bf16[8,8,1,4096]{3,1,2,0:T(8,128)(2,1)} %stack.10), calls=%async_computation.2 | async-start | bytes 1048576 | tf_op jit(solution)/shard_map/all_to_all | solution.py:44
  285.1 15.9 %all-to-all-done.2 = bf16[8,8,1,4096]{3,1,2,0:T(8,128)(2,1)S(1)} async-done(((bf16[8,8,1,4096]{3,1,2,0:T(8,128)(2,1)}), bf16[8,8,1,4096]{3,1,2,0:T(8,128)(2,1)S(1)}, u32[]{:S(2)}, u32[]{:S(2)}) %all-to-all-start.2) | async-done | bytes 524320 | tf_op jit(solution)/shard_map/all_to_all | solution.py:44
  301.1 6.0 %all_to_all.63 = bf16[2,64,1,4096]{3,1,2,0:T(8,128)(2,1)S(1)} all-to-all(bf16[2,64,1,4096]{3,1,2,0:T(8,128)(2,1)S(1)} %pad_maximum_fusion), channel_id=1, replica_groups=mesh['grp'=2,'pool_0'=8,'pool_1'=8,'pool_2'=2] {'pool_2'}, dimensions={0} | all-to-all | bytes 2097152 | tf_op jit(solution)/shard_map/all_to_all | solution.py:44
  309.2 2.4 reshape_reshape.7
  313.5 19.1 %all_to_all.64 = bf16[128,1,64]{2,1,0:T(2,128)(2,1)S(1)} all-to-all(bf16[128,1,64]{2,1,0:T(2,128)(2,1)S(1)} %copy.144), channel_id=1, replica_groups=mesh['grp'=2,'pool_0'=8,'pool_1'=8,'pool_2'=2] {'pool_0','pool_1','pool_2'}, dimensions={0} | all-to-all | bytes 32768 | tf_op jit(solution)/shard_map/all_to_all | solution.py:136
  (58 shorter events, 24.6 us)
Async XLA Ops:
  6.5 70.4 %copy-start = (bf16[64,2,16,512]{3,2,1,0:T(8,128)(2,1)S(1)}, bf16[64,2,16,512]{3,2,1,0:T(8,128)(2,1)}, u32[]{:S(2)}) copy-start(bf16[64,2,16,512]{3,2,1,0:T(8,128)(2,1)} %param.7) | copy-start | bytes 6291460
  6.6 117.5 %all-gather.4.cloned.1.call-start = ((), (), s32[]{:S(2)}) async-start(), calls=%async_computation.6 | async-start | bytes 2113536 | tf_op jit(solution)/shard_map/all_gather | solution.py:105
  231.7 11.6 %copy-start.2 = (bf16[32,8192]{1,0:T(8,128)(2,1)S(1)}, bf16[32,8192]{1,0:T(8,128)(2,1)}, u32[]{:S(2)}) copy-start(bf16[32,8192]{1,0:T(8,128)(2,1)} %param.11) | copy-start | bytes 1572868
  239.1 11.5 %all-to-all-start.1 = ((bf16[8,2,2048]{2,1,0:T(2,128)(2,1)}), bf16[8,2,2048]{2,1,0:T(2,128)(2,1)S(1)}, u32[]{:S(2)}, u32[]{:S(2)}) async-start(bf16[8,2,2048]{2,1,0:T(2,128)(2,1)} %reshape.140), calls=%async_computation.1 | async-start | bytes 131072 | tf_op jit(solution)/shard_map/all_to_all | solution.py:44
  250.6 29.4 %all-to-all-start.4 = ((bf16[128,2,1024]{2,1,0:T(2,128)(2,1)}), bf16[128,2,1024]{2,1,0:T(2,128)(2,1)S(1)}, u32[]{:S(2)}, u32[]{:S(2)}) async-start(bf16[128,2,1024]{2,1,0:T(2,128)(2,1)} %reshape.142), calls=%async_computation.4 | async-start | bytes 1048576 | tf_op jit(solution)/shard_map/all_to_all | solution.py:131
  280.8 20.2 %all-to-all-start.2 = ((bf16[8,8,1,4096]{3,1,2,0:T(8,128)(2,1)}), bf16[8,8,1,4096]{3,1,2,0:T(8,128)(2,1)S(1)}, u32[]{:S(2)}, u32[]{:S(2)}) async-start(bf16[8,8,1,4096]{3,1,2,0:T(8,128)(2,1)} %stack.10), calls=%async_computation.2 | async-start | bytes 1048576 | tf_op jit(solution)/shard_map/all_to_all | solution.py:44
  309.2 24.3 %copy-start.1 = (bf16[64,2,16,512]{3,2,1,0:T(8,128)(2,1)S(1)}, bf16[64,2,16,512]{3,2,1,0:T(8,128)(2,1)}, u32[]{:S(2)}) copy-start(bf16[64,2,16,512]{3,2,1,0:T(8,128)(2,1)} %param.7) | copy-start | bytes 6291460
Sparse Core Ops, SparseCore 0:
  9.9 98.6 all-gather.3
